TPU v7x, 32 devices: a whole 2x2x4 slice. The times are simulated.
32 devices in a mesh: swath: 2 (over x), band: 16 (over z, y, core).
Axes of the slice: x: 2, y: 2, z: 4, core: 2. Of those that a mesh axis runs over, the one named last changes fastest.
Arguments:
- design: bfloat16 [512, 16384], P(('swath', 'band')), parts along dimension 0, may hold values from 0 to 1
- row_taps: bfloat16 [8, 33], replicated, may hold values from -1 to 1
- column_taps: bfloat16 [8, 33], replicated, may hold values from -1 to 1
- kernel_weight: float32 [8], replicated, may hold values from 0.5 to 2
- interp: bfloat16 [32, 8], replicated, may hold values from 0 to 0.29882812
- block_shift: int32 [2, 4, 16], P(None, 'swath', 'band'), parts along dimension 1, may hold values from -24 to 24
- block_phase: int32 [2, 4, 16], P(None, 'swath', 'band'), parts along dimension 1, may hold values from 0 to 31
- care: int32 [4, 16], P('swath', 'band'), parts along dimension 0, may hold values 0 or 1
- image: bfloat16 [512, 16384], P('swath', 'band'), parts along dimension 0, may hold values from 0 to 20, as said below
Outputs:
- diff_map: bfloat16 [512, 16384], P('swath', 'band'), parts along dimension 0
There are 2 independent parts, one for each index of `swath`. A program takes and returns all parts, laid end to end along the dimension named above; an argument that names none is the same for every part. Nothing has to cross between parts.
Inputs may be any that keep to these rules, and one draw needn't show every extreme that they name: `image`: nonnegative intensities.
All inputs are finite; a program needn't handle non-finite values. No bound on the sum of `care` on one device may be relied on, other than what follows from the above.
Results may differ from a plain program's by a relative error of at most 0.0045.
Values may be sent and summed in bfloat16 or wider, within the bound.
A program may use at most 64 MiB of HBM per device.

v0:
```python
import jax
import jax.numpy as jnp
from jax import lax
from jax.sharding import PartitionSpec as P

NK = 8
KH = 16
IH = 4
NF = 32
BLK = 128
P_SIZE = 28


epsilon = 1e-05
panel = 128


def padded_2(cells, sides, width):
    for axis, dim in sides:
        count = lax.axis_size(axis)
        ends = count - 1
        head = lax.slice_in_dim(cells, 0, width, axis=dim)
        tail = lax.slice_in_dim(cells, cells.shape[dim] - width, cells.shape[dim], axis=dim)
        cells = jnp.concatenate(
            [
                lax.ppermute(tail, axis, [(i, (i + 1) % count) for i in range(ends)]),
                cells,
                lax.ppermute(head, axis, [((i + 1) % count, i) for i in range(ends)]),
            ],
            axis=dim,
        )
    return cells


def band_matrix(offsets, phases, interp, size_out, size_in):
    table = jax.nn.one_hot(phases, NF, dtype=jnp.float32)
    weights = jnp.dot(table, interp.astype(jnp.float32), precision=lax.Precision.HIGHEST)
    outer = jnp.arange(size_out, dtype=jnp.int32)
    inner = jnp.arange(size_in, dtype=jnp.int32)
    position = (
        inner[None, None, :] - outer[None, :, None] - offsets[:, None, None] + (IH - 1 - P_SIZE)
    )
    matrix = jnp.zeros(position.shape, jnp.float32)
    for tap in range(2 * IH):
        matrix = matrix + jnp.where(position == tap, weights[:, tap][:, None, None], 0.0)
    return matrix.astype(jnp.bfloat16)


def warp_strip(framed, shifts, phases, interp):
    height = framed.shape[0] - BLK - 2 * P_SIZE
    across = framed.shape[1]
    strip_cols = across - 2 * P_SIZE
    count = height // BLK
    upper = framed[:height].reshape(count, BLK, across)[:, :P_SIZE]
    middle = framed[P_SIZE : P_SIZE + height].reshape(count, BLK, across)
    lower = framed[BLK + P_SIZE : BLK + P_SIZE + height].reshape(count, BLK, across)[:, :P_SIZE]
    blocks = jnp.concatenate([upper, middle, lower], axis=1)
    row_matrix = band_matrix(shifts[0], phases[0], interp, BLK, BLK + 2 * P_SIZE)
    column_matrix = band_matrix(shifts[1], phases[1], interp, strip_cols, across)
    partial_value = jnp.einsum(
        "brs,bsc->brc", row_matrix, blocks, preferred_element_type=jnp.float32
    ).astype(jnp.bfloat16)
    return jnp.einsum(
        "brs,bcs->brc", partial_value, column_matrix, preferred_element_type=jnp.float32
    )


def on_device(
    design, row_taps, column_taps, kernel_weight, interp, block_shift, block_phase, care, image
):
    devices = lax.axis_size("band")
    rows_dev, width = design.shape
    strip_cols = width // devices
    reach = row_taps.shape[1]
    extended = padded_2(design, (("band", 0),), KH)
    row_offsets = jnp.arange(rows_dev + 2 * KH)[None, :] - jnp.arange(rows_dev)[:, None]
    row_selector = (row_offsets[:, :, None] == jnp.arange(reach)[None, None, :]).astype(
        jnp.bfloat16
    )
    row_mats = jnp.einsum(
        "rst,kt->krs", row_selector, row_taps, preferred_element_type=jnp.float32
    ).astype(jnp.bfloat16)
    window = panel + 2 * KH
    column_offsets = jnp.arange(window)[:, None] - jnp.arange(panel)[None, :]
    column_selector = (column_offsets[:, :, None] == jnp.arange(reach)[None, None, :]).astype(
        jnp.bfloat16
    )
    column_mats = jnp.einsum(
        "ict,kt->kic", column_selector, column_taps, preferred_element_type=jnp.float32
    ).astype(jnp.bfloat16)
    panels = width // panel
    total = jnp.zeros((rows_dev, width), jnp.float32)
    for kernel in range(NK):
        smoothed = jnp.dot(row_mats[kernel], extended, preferred_element_type=jnp.float32).astype(
            jnp.bfloat16
        )
        framed = jnp.pad(smoothed, ((0, 0), (panel, panel))).reshape(rows_dev, panels + 2, panel)
        stacked = jnp.concatenate(
            [framed[:, :-2, panel - KH :], framed[:, 1:-1], framed[:, 2:, :KH]], axis=2
        )
        field = jnp.einsum(
            "rnj,jc->rnc", stacked, column_mats[kernel], preferred_element_type=jnp.float32
        ).reshape(rows_dev, width)
        total = total + kernel_weight[kernel] * field * field
    intensity = total.astype(jnp.bfloat16)
    height = rows_dev * devices
    strip = lax.all_to_all(intensity, "band", split_axis=1, concat_axis=0, tiled=True)
    bordered = padded_2(strip, (("band", 1),), P_SIZE)
    padded = jnp.pad(bordered, ((P_SIZE, BLK + P_SIZE), (0, 0)))
    warped = warp_strip(padded, block_shift[:, :, 0], block_phase[:, :, 0], interp)
    count = height // BLK
    care_blocks = care[:, 0].astype(jnp.float32)
    measured = image.reshape(count, BLK, strip_cols).astype(jnp.float32)
    difference = (care_blocks[:, None, None] * (measured - warped)).reshape(height, strip_cols)
    shifted = jnp.pad(difference, ((1, 1), (0, 0)))
    filtered = difference + 0.5 * (shifted[:-2] + shifted[2:])
    cells = height * width
    first_sum, second_sum = lax.psum((jnp.sum(filtered), jnp.sum(filtered * filtered)), "band")
    mean = first_sum / cells
    variance = second_sum / cells - mean * mean
    centered = filtered - mean
    scaled = (centered * lax.rsqrt(variance + epsilon)).reshape(count, BLK, strip_cols)
    return (care_blocks[:, None, None] * scaled).reshape(height, strip_cols).astype(jnp.bfloat16)


def solution(mesh):
    placed = (
        P(("swath", "band"), None),
        P(),
        P(),
        P(),
        P(),
        P(None, "swath", "band"),
        P(None, "swath", "band"),
        P("swath", "band"),
        P("swath", "band"),
    )
    return jax.shard_map(
        on_device, mesh=mesh, in_specs=placed, out_specs=P("swath", "band"), check_vma=False
    )
```

profile of v0, /device:TPU:0, one launch (start us, length us, event | category | flops | bytes accessed | tf_op | source)
XLA Modules:
  0.0 193.9 jit_solution(986255994731446772)
XLA Ops:
  0.0 2.6 %collective-permute-start = (bf16[16,16384]{1,0:T(8,128)(2,1)}, bf16[16,16384]{1,0:T(8,128)(2,1)S(1)}, u32[]{:S(2)}, u32[]{:S(2)}) collective-permute-start(bf16[16,16384]{1,0:T(8,128)(2,1)} %param.9), channel_id=1, source_target_pairs={{0,1},{1,2},{2,3},{3,4},{4,5},{5,6},{6,7},{7,8},{8,9},{9,10},{10,1... | collective-permute-start | bytes 1572872 | tf_op jit(solution)/shard_map/ppermute | solution.py:26
  8.6 1.6 fusion.215
  35.1 1.5 fusion.34
  39.6 2.5 %fusion.40 = f32[16,128,128]{2,1,0:T(8,128)} fusion(bf16[16,128,16]{1,2,0:T(8,128)(2,1)S(1)} %copy.95, bf16[16,128,128]{1,2,0:T(8,128)(2,1)} %copy.94, bf16[16,128,16]{1,2,0:T(8,128)(2,1)S(1)} %copy.93, bf16[1,160,128]{2,0,1:T(2,128)(2,1)} %get-tuple-element.53), kind=kOutput, calls=%fused_computation.62 | convolution fusion | flops 85852160 | bytes 1744896 | tf_op jit(solution)/shard_map/rnj,jc->rnc/dot_general | solution.py:101
  46.0 2.5 %fusion.46 = f32[16,128,128]{2,1,0:T(8,128)} fusion(bf16[16,128,16]{1,2,0:T(8,128)(2,1)S(1)} %copy.98, bf16[16,128,128]{1,2,0:T(8,128)(2,1)} %copy.97, bf16[16,128,16]{1,2,0:T(8,128)(2,1)S(1)} %copy.96, bf16[1,160,128]{2,0,1:T(2,128)(2,1)} %get-tuple-element.52), kind=kOutput, calls=%fused_computation.68 | convolution fusion | flops 85852160 | bytes 1744896 | tf_op jit(solution)/shard_map/rnj,jc->rnc/dot_general | solution.py:101
  49.9 2.0 %copy.100 = bf16[16,128,128]{1,2,0:T(8,128)(2,1)} copy(bf16[16,128,128]{2,1,0:T(8,128)(2,1)} %slice.326) | data formatting | bytes 1048576
  52.0 1.8 copy.99
  53.8 1.8 copy.101
  55.6 2.6 %fusion.52 = f32[16,128,128]{2,1,0:T(8,128)} fusion(bf16[16,128,16]{1,2,0:T(8,128)(2,1)} %copy.101, bf16[16,128,128]{1,2,0:T(8,128)(2,1)} %copy.100, bf16[16,128,16]{1,2,0:T(8,128)(2,1)} %copy.99, bf16[1,160,128]{2,0,1:T(2,128)(2,1)} %get-tuple-element.51), kind=kOutput, calls=%fused_computation.74 | convolution fusion | flops 85852160 | bytes 1744896 | tf_op jit(solution)/shard_map/rnj,jc->rnc/dot_general | solution.py:101
  58.3 2.4 %reshape.176 = f32[16,16,1024]{2,1,0:T(8,128)} reshape(f32[16,128,128]{2,1,0:T(8,128)} %fusion.52) | data formatting | bytes 2097152 | tf_op jit(solution)/shard_map/reshape | solution.py:103
  60.6 2.1 %copy.103 = bf16[16,128,128]{1,2,0:T(8,128)(2,1)} copy(bf16[16,128,128]{2,1,0:T(8,128)(2,1)} %slice.331) | data formatting | bytes 1048576
  62.7 1.8 copy.102
  64.5 1.8 copy.104
  66.4 2.6 %fusion.58 = f32[16,128,128]{2,1,0:T(8,128)} fusion(bf16[16,128,16]{1,2,0:T(8,128)(2,1)} %copy.104, bf16[16,128,128]{1,2,0:T(8,128)(2,1)} %copy.103, bf16[16,128,16]{1,2,0:T(8,128)(2,1)} %copy.102, bf16[1,160,128]{2,0,1:T(2,128)(2,1)S(1)} %get-tuple-element.50), kind=kOutput, calls=%fused_computation.80 | convolution fusion | flops 85852160 | bytes 1744896 | tf_op jit(solution)/shard_map/rnj,jc->rnc/dot_general | solution.py:101
  68.9 2.4 %reshape.178 = f32[16,16,1024]{2,1,0:T(8,128)} reshape(f32[16,128,128]{2,1,0:T(8,128)} %fusion.58) | data formatting | bytes 2097152 | tf_op jit(solution)/shard_map/reshape | solution.py:103
  71.4 2.0 %copy.106 = bf16[16,128,128]{1,2,0:T(8,128)(2,1)} copy(bf16[16,128,128]{2,1,0:T(8,128)(2,1)} %slice.336) | data formatting | bytes 1048576
  74.6 1.8 copy.107
  76.5 2.6 %fusion.64 = f32[16,128,128]{2,1,0:T(8,128)} fusion(bf16[16,128,16]{1,2,0:T(8,128)(2,1)} %copy.107, bf16[16,128,128]{1,2,0:T(8,128)(2,1)} %copy.106, bf16[16,128,16]{1,2,0:T(8,128)(2,1)S(1)} %copy.105, bf16[1,160,128]{2,0,1:T(2,128)(2,1)S(1)} %get-tuple-element.49), kind=kOutput, calls=%fused_computation.86 | convolution fusion | flops 85852160 | bytes 1744896 | tf_op jit(solution)/shard_map/rnj,jc->rnc/dot_general | solution.py:101
  79.0 2.4 %reshape.180 = f32[16,16,1024]{2,1,0:T(8,128)} reshape(f32[16,128,128]{2,1,0:T(8,128)} %fusion.64) | data formatting | bytes 2097152 | tf_op jit(solution)/shard_map/reshape | solution.py:103
  81.4 2.0 %copy.109 = bf16[16,128,128]{1,2,0:T(8,128)(2,1)} copy(bf16[16,128,128]{2,1,0:T(8,128)(2,1)} %slice.341) | data formatting | bytes 1048576
  85.9 2.5 %fusion.70 = f32[16,128,128]{2,1,0:T(8,128)} fusion(bf16[16,128,16]{1,2,0:T(8,128)(2,1)S(1)} %copy.110, bf16[16,128,128]{1,2,0:T(8,128)(2,1)} %copy.109, bf16[16,128,16]{1,2,0:T(8,128)(2,1)S(1)} %copy.108, bf16[1,160,128]{2,0,1:T(2,128)(2,1)S(1)} %get-tuple-element.48), kind=kOutput, calls=%fused_computation.92 | convolution fusion | flops 85852160 | bytes 1744896 | tf_op jit(solution)/shard_map/rnj,jc->rnc/dot_general | solution.py:101
  88.4 2.4 %reshape.182 = f32[16,16,1024]{2,1,0:T(8,128)} reshape(f32[16,128,128]{2,1,0:T(8,128)} %fusion.70) | data formatting | bytes 2097152 | tf_op jit(solution)/shard_map/reshape | solution.py:103
  90.8 2.0 %copy.112 = bf16[16,128,128]{1,2,0:T(8,128)(2,1)} copy(bf16[16,128,128]{2,1,0:T(8,128)(2,1)} %slice.346) | data formatting | bytes 1048576
  95.2 2.6 %fusion.76 = f32[16,128,128]{2,1,0:T(8,128)} fusion(bf16[16,128,16]{1,2,0:T(8,128)(2,1)S(1)} %copy.113, bf16[16,128,128]{1,2,0:T(8,128)(2,1)} %copy.112, bf16[16,128,16]{1,2,0:T(8,128)(2,1)S(1)} %copy.111, bf16[1,160,128]{2,0,1:T(2,128)(2,1)S(1)} %get-tuple-element.47), kind=kOutput, calls=%fused_computation.98 | convolution fusion | flops 85852160 | bytes 1744896 | tf_op jit(solution)/shard_map/rnj,jc->rnc/dot_general | solution.py:101
  97.8 2.4 %reshape.184 = f32[16,16,1024]{2,1,0:T(8,128)} reshape(f32[16,128,128]{2,1,0:T(8,128)} %fusion.76) | data formatting | bytes 2097152 | tf_op jit(solution)/shard_map/reshape | solution.py:103
  100.2 13.3 %fusion.23 = bf16[16,16,1024]{2,0,1:T(8,128)(2,1)} fusion(f32[16,16,1024]{2,1,0:T(8,128)} %reshape.184, f32[16,16,1024]{2,1,0:T(8,128)} %reshape.182, f32[16,16,1024]{2,1,0:T(8,128)} %reshape.180, f32[16,16,1024]{2,1,0:T(8,128)} %reshape.178, f32[16,16,1024]{2,1,0:T(8,128)} %reshape.176, f32[16,16,1024]{2,1,0:T(8,128)S(1)} %reshape.174, ...), kind=kLoop, calls=%fused_computation.47 | loop fusion | flops 6291456 | bytes 8912928 | tf_op jit(solution)/shard_map/convert_element_type | solution.py:105
  113.4 11.0 %all-to-all-start = ((bf16[16,16,1024]{2,0,1:T(8,128)(2,1)}), bf16[16,16,1024]{2,0,1:T(8,128)(2,1)S(1)}, u32[]{:S(2)}, u32[]{:S(2)}) async-start(bf16[16,16,1024]{2,0,1:T(8,128)(2,1)} %fusion.23), calls=%async_computation | async-start | bytes 1048576 | tf_op jit(solution)/shard_map/all_to_all | solution.py:107
  124.9 2.6 %iota_subtract_fusion = s32[1024,1080]{0,1:T(8,128)} fusion(), kind=kLoop, calls=%fused_computation.18 | loop fusion | flops 1105920 | bytes 4423680 | tf_op jit(solution)/shard_map/sub | solution.py:41
  127.5 11.2 %all-to-all-done = bf16[16,16,1024]{2,0,1:T(8,128)(2,1)S(1)} async-done(((bf16[16,16,1024]{2,0,1:T(8,128)(2,1)}), bf16[16,16,1024]{2,0,1:T(8,128)(2,1)S(1)}, u32[]{:S(2)}, u32[]{:S(2)}) %all-to-all-start) | async-done | bytes 524320 | tf_op jit(solution)/shard_map/all_to_all | solution.py:107
  140.1 3.0 %collective-permute-start.2 = (bf16[256,28]{1,0:T(8,128)(2,1)S(1)}, bf16[256,28]{1,0:T(8,128)(2,1)S(1)}, u32[]{:S(2)}, u32[]{:S(2)}) collective-permute-start(bf16[256,28]{1,0:T(8,128)(2,1)S(1)} %get-tuple-element.45), channel_id=1, source_target_pairs={{0,1},{1,2},{2,3},{3,4},{4,5},{5,6},{6,7},{7,8},{8,9},{9,10},{10,1... | collective-permute-start | bytes 43016 | tf_op jit(solution)/shard_map/ppermute | solution.py:26
  145.7 10.7 %fusion.12 = f32[2,128,1024]{2,1,0:T(8,128)S(1)} fusion(f32[2]{0:T(128)S(1)} %get-tuple-element.16, f32[2]{0:T(128)S(1)} %get-tuple-element.17, f32[2]{0:T(128)S(1)} %get-tuple-element.18, f32[2]{0:T(128)S(1)} %get-tuple-element.19, f32[2]{0:T(128)S(1)} %get-tuple-element.20, f32[2]{0:T(128)S(1)} %get-tuple-element.21, f32[2]{0:T(128)S(1)} %get-tuple-element.22, ...), kind=kOutput, calls=%fused_computation.33 | convolution fusion | flops 730155776 | bytes 6885784 | tf_op jit(solution)/shard_map/brs,bcs->brc/dot_general | solution.py:63
  157.6 32.8 %all-reduce.10 = (f32[]{:T(128)}, f32[]{:T(128)}) all-reduce(f32[]{:T(128)} %get-tuple-element.6, f32[]{:T(128)} %get-tuple-element.5), channel_id=1, replica_groups=mesh['swath'=2,'band'=16] {'band'}, use_global_device_ids=true, to_apply=%region_3.4 | all-reduce | flops 2 | bytes 16 | tf_op jit(solution)/shard_map/psum | solution.py:118
  (126 shorter events, 51.3 us)
Async XLA Ops:
  0.0 10.2 %copy-start = (bf16[8,33]{1,0:T(8,128)(2,1)S(1)}, bf16[8,33]{1,0:T(8,128)(2,1)}, u32[]{:S(2)}) copy-start(bf16[8,33]{1,0:T(8,128)(2,1)} %param.11) | copy-start | bytes 1588
  0.0 12.1 %collective-permute-start = (bf16[16,16384]{1,0:T(8,128)(2,1)}, bf16[16,16384]{1,0:T(8,128)(2,1)S(1)}, u32[]{:S(2)}, u32[]{:S(2)}) collective-permute-start(bf16[16,16384]{1,0:T(8,128)(2,1)} %param.9), channel_id=1, source_target_pairs={{0,1},{1,2},{2,3},{3,4},{4,5},{5,6},{6,7},{7,8},{8,9},{9,10},{10,1... | collective-permute-start | bytes 1572872 | tf_op jit(solution)/shard_map/ppermute | solution.py:26
  2.6 9.7 %collective-permute-start.1 = (bf16[16,16384]{1,0:T(8,128)(2,1)}, bf16[16,16384]{1,0:T(8,128)(2,1)S(1)}, u32[]{:S(2)}, u32[]{:S(2)}) collective-permute-start(bf16[16,16384]{1,0:T(8,128)(2,1)} %param.9), channel_id=1, source_target_pairs={{1,0},{2,1},{3,2},{4,3},{5,4},{6,5},{7,6},{8,7},{9,8},{10,9},{11,1... | collective-permute-start | bytes 1572872 | tf_op jit(solution)/shard_map/ppermute | solution.py:28
  4.6 5.7 %copy-start.17 = (f32[2]{0:T(128)}, f32[2]{0:T(128)S(1)}, u32[]{:S(2)}) copy-start(f32[2]{0:T(128)S(1)} %convert_bitcast_fusion) | copy-start | bytes 28
  10.2 1.9 %copy-start.8 = (bf16[16,16384]{1,0:T(8,128)(2,1)S(1)}, bf16[16,16384]{1,0:T(8,128)(2,1)}, u32[]{:S(2)}) copy-start(bf16[16,16384]{1,0:T(8,128)(2,1)} %param.9) | copy-start | bytes 1572868
  18.8 1.3 copy-start.10
  32.0 2.2 %copy-start.2 = (bf16[16,128,128]{2,1,0:T(8,128)(2,1)S(1)}, bf16[16,128,128]{2,1,0:T(8,128)(2,1)}, u32[]{:S(2)}) copy-start(bf16[16,128,128]{2,1,0:T(8,128)(2,1)} %slice.311) | copy-start | bytes 1572868
  33.0 1.5 copy-start.7
  33.0 1.7 copy-start.6
  34.2 0.9 copy-start.9
  35.1 3.0 %copy-start.1 = (bf16[16,128,128]{2,1,0:T(8,128)(2,1)S(1)}, bf16[16,128,128]{2,1,0:T(8,128)(2,1)}, u32[]{:S(2)}) copy-start(bf16[16,128,128]{2,1,0:T(8,128)(2,1)} %slice.316) | copy-start | bytes 1572868
  36.6 2.6 %copy-start.5 = (bf16[16,128,16]{2,1,0:T(8,128)(2,1)S(1)}, bf16[16,128,16]{2,1,0:T(8,128)(2,1)}, u32[]{:S(2)}) copy-start(bf16[16,128,16]{2,1,0:T(8,128)(2,1)} %get-tuple-element.30) | copy-start | bytes 196612
  36.6 2.8 %copy-start.4 = (bf16[16,128,16]{2,1,0:T(8,128)(2,1)S(1)}, bf16[16,128,16]{2,1,0:T(8,128)(2,1)}, u32[]{:S(2)}) copy-start(bf16[16,128,16]{2,1,0:T(8,128)(2,1)} %get-tuple-element.31) | copy-start | bytes 196612
  42.1 3.7 %copy-start.3 = (bf16[16,128,16]{2,1,0:T(8,128)(2,1)S(1)}, bf16[16,128,16]{2,1,0:T(8,128)(2,1)}, u32[]{:S(2)}) copy-start(bf16[16,128,16]{2,1,0:T(8,128)(2,1)} %get-tuple-element.33) | copy-start | bytes 196612
  100.2 24.3 %copy-start.14 = (s32[2]{0:T(128)S(1)}, s32[2]{0:T(128)}, u32[]{:S(2)}) copy-start(s32[2]{0:T(128)} %get-tuple-element.64) | copy-start | bytes 28
  100.2 24.3 %copy-start.16 = (bf16[32,8]{0,1:T(8,128)(2,1)S(1)}, bf16[32,8]{0,1:T(8,128)(2,1)}, u32[]{:S(2)}) copy-start(bf16[32,8]{0,1:T(8,128)(2,1)} %param.13) | copy-start | bytes 1540
  100.2 24.5 %copy-start.13 = (s32[2]{0:T(128)S(1)}, s32[2]{0:T(128)}, u32[]{:S(2)}) copy-start(s32[2]{0:T(128)} %get-tuple-element.65) | copy-start | bytes 28
  113.4 25.3 %all-to-all-start = ((bf16[16,16,1024]{2,0,1:T(8,128)(2,1)}), bf16[16,16,1024]{2,0,1:T(8,128)(2,1)S(1)}, u32[]{:S(2)}, u32[]{:S(2)}) async-start(bf16[16,16,1024]{2,0,1:T(8,128)(2,1)} %fusion.23), calls=%async_computation | async-start | bytes 1048576 | tf_op jit(solution)/shard_map/all_to_all | solution.py:107
  138.8 4.8 %collective-permute-start.3 = (bf16[256,28]{1,0:T(8,128)(2,1)S(1)}, bf16[256,28]{1,0:T(8,128)(2,1)S(1)}, u32[]{:S(2)}, u32[]{:S(2)}) collective-permute-start(bf16[256,28]{1,0:T(8,128)(2,1)S(1)} %get-tuple-element.44), channel_id=1, source_target_pairs={{1,0},{2,1},{3,2},{4,3},{5,4},{6,5},{7,6},{8,7},{9,8},{10,9},{11,1... | collective-permute-start | bytes 43016 | tf_op jit(solution)/shard_map/ppermute | solution.py:28
  140.1 3.9 %collective-permute-start.2 = (bf16[256,28]{1,0:T(8,128)(2,1)S(1)}, bf16[256,28]{1,0:T(8,128)(2,1)S(1)}, u32[]{:S(2)}, u32[]{:S(2)}) collective-permute-start(bf16[256,28]{1,0:T(8,128)(2,1)S(1)} %get-tuple-element.45), channel_id=1, source_target_pairs={{0,1},{1,2},{2,3},{3,4},{4,5},{5,6},{6,7},{7,8},{8,9},{9,10},{10,1... | collective-permute-start | bytes 43016 | tf_op jit(solution)/shard_map/ppermute | solution.py:26
  144.6 0.9 copy-start.11
  144.7 0.9 copy-start.12
  144.7 1.0 copy-start.15
  144.7 1.0 copy-start.18
where the time goes:
time: 196 us; the launch traced here: 194 us
  local copies, waits for them, and re-layouts  73.8 us (38%)
  matrix products  34.7 us (18%)
  blocking collectives  32.8 us (17%)
  starting transfers between devices  19.2 us (10%)
  other arithmetic  18.7 us (10%)
  waiting for transfers between devices  11.7 us (6%)
  between operations  3.08 us (2%)
    psum x1, blocking collectives, on_device(): lax.psum((jnp.sum(filtered), jnp.sum(filtered * filtered)), 'band')  32.8 us
    unnamed x64, local copies, waits for them, and re-layouts  30.6 us
    dot_general x8, matrix products, on_device(): jnp.einsum('rnj,jc->rnc', stacked, column_mats[kernel], preferred_element...  19.4 us
    reshape x8, local copies, waits for them, and re-layouts, on_device(): field = jnp.einsum('rnj,jc->rnc', stacked, column_mats[kernel], preferred...  16.2 us
    convert_element_type x1, other arithmetic, on_device(): intensity = total.astype(jnp.bfloat16)  13.3 us
    all_to_all x1, waiting for transfers between devices, on_device(): lax.all_to_all(intensity, 'band', split_axis=1, concat_axis=0, tiled=True)  11.2 us
    all_to_all x1, starting transfers between devices, on_device(): lax.all_to_all(intensity, 'band', split_axis=1, concat_axis=0, tiled=True)  11 us
    dot_general x1, matrix products, warp_strip(): jnp.einsum('brs,bcs->brc', partial_value, column_matrix, preferred_elemen...  10.7 us
  transfers between devices with their start and end apart: 5, of which 2 were waited for; matrix products, arithmetic and copies ran while one was open for 6% of the time, Pallas kernels for 0%

commit v1 on v0

v1 whole, which is shorter than its diff:
```python
import functools

import jax
import jax.numpy as jnp
from jax import lax
from jax.experimental import pallas as pl
from jax.experimental.pallas import tpu as pltpu
from jax.sharding import PartitionSpec as P

NK = 8
KH = 16
IH = 4
BLK = 128
P_SIZE = 28
LANES = 128
EDGE = 32
GROUP = 4
REACH = 2 * KH + 1

epsilon = 1e-05
F32 = jnp.float32
BF16 = jnp.bfloat16


def banded(offset, taps, shape):
    place = (
        lax.broadcasted_iota(jnp.int32, shape, 0)
        - lax.broadcasted_iota(jnp.int32, shape, 1)
        - offset
    )
    matrix = jnp.zeros(shape, F32)
    for tap in range(taps.shape[1]):
        matrix = jnp.where(place == tap, taps[:, tap : tap + 1], matrix)
    return matrix


def banded_rows(offset, taps, shape):
    place = (
        lax.broadcasted_iota(jnp.int32, shape, 1)
        - lax.broadcasted_iota(jnp.int32, shape, 0)
        - offset
    )
    matrix = jnp.zeros(shape, F32)
    for tap in range(taps.shape[1]):
        matrix = jnp.where(place == tap, taps[:, tap : tap + 1], matrix)
    return matrix


def kernel(
    n, height, width,
    weight_ref, shift_ref, phase_ref, care_ref,
    design_ref, row_ref, column_ref, interp_ref, image_hbm,
    out_ref,
    sendbuf, recv, image, row_mats, column_mats, taps, table, smooth, intensity,
    diff, filt, stats_mine, stats_all,
    send_sem, recv_sem, stat_send, stat_recv, image_sem,
):
    me = lax.axis_index("band")
    rows = design_ref.shape[0]
    strip = width // n
    panels = strip // LANES
    wide = strip + LANES
    block_rows = GROUP * rows
    window = block_rows + 2 * KH
    steps = n // GROUP

    barrier = pltpu.get_barrier_semaphore()

    def greet(i, carry):
        peer = lax.rem(me + i, n)
        pl.semaphore_signal(
            barrier, inc=1, device_id={"band": peer}, device_id_type=pl.DeviceIdType.MESH
        )
        return carry

    lax.fori_loop(1, n, greet, 0)

    fetch = pltpu.make_async_copy(image_hbm, image, image_sem)
    fetch.start()

    lane = lax.broadcasted_iota(jnp.int32, (rows, LANES), 1)
    low = lane < LANES // 2
    zero_panel = jnp.zeros((rows, LANES), BF16)
    for owner in range(n):
        start = owner * strip
        sendbuf[owner, :, :strip] = design_ref[:, start : start + strip]
        after = design_ref[:, start + strip : start + strip + LANES] if owner < n - 1 else zero_panel
        before = design_ref[:, start - LANES : start] if owner > 0 else zero_panel
        sendbuf[owner, :, strip:] = jnp.where(low, after, before)

    pl.semaphore_wait(barrier, n - 1)

    def copy_to(peer):
        return pltpu.make_async_remote_copy(
            src_ref=sendbuf.at[peer],
            dst_ref=recv.at[pl.ds(pl.multiple_of(KH + me * rows, rows), rows), :],
            send_sem=send_sem.at[peer],
            recv_sem=recv_sem.at[me],
            device_id={"band": peer},
            device_id_type=pl.DeviceIdType.MESH,
        )

    def copy_from(peer):
        return pltpu.make_async_remote_copy(
            src_ref=sendbuf.at[peer],
            dst_ref=recv.at[pl.ds(pl.multiple_of(KH + peer * rows, rows), rows), :],
            send_sem=send_sem.at[peer],
            recv_sem=recv_sem.at[peer],
            device_id={"band": peer},
            device_id_type=pl.DeviceIdType.MESH,
        )

    def send(i, carry):
        peer = lax.rem(me + n // 2 + i, n)

        @pl.when(peer != me)
        def _():
            copy_to(peer).start()

        return carry

    lax.fori_loop(0, n, send, 0)

    recv[pl.ds(pl.multiple_of(KH + me * rows, rows), rows), :] = sendbuf[me]
    recv[:KH, :] = jnp.zeros((KH, wide), BF16)
    recv[KH + height :, :] = jnp.zeros((KH, wide), BF16)
    intensity[:EDGE, :] = jnp.zeros((EDGE, wide), BF16)
    intensity[EDGE + height :, :] = jnp.zeros((EDGE, wide), BF16)
    diff[:8, :] = jnp.zeros((8, strip), F32)
    diff[8 + height :, :] = jnp.zeros((8, strip), F32)

    taps[:NK, :REACH] = row_ref[...].astype(F32)
    taps[NK:, :REACH] = column_ref[...].astype(F32)
    table[:, : 2 * IH] = interp_ref[...].astype(F32)

    def build(k, carry):
        row_taps = taps[pl.ds(k, 1), :REACH]
        row_mats[pl.ds(pl.multiple_of(k * block_rows, block_rows), block_rows), :] = banded_rows(
            0, row_taps, (block_rows, window)
        ).astype(BF16)
        column_taps = taps[pl.ds(NK + k, 1), :REACH]
        column_mats[k] = banded(LANES - P_SIZE - KH, column_taps, (2 * LANES, LANES)).astype(BF16)
        return carry

    lax.fori_loop(0, NK, build, 0)

    rising = me < n // 2

    def arrived(place):
        band = jnp.where(rising, place, n - 1 - place)

        @pl.when(jnp.logical_and(place < n, band != me))
        def _():
            copy_from(band).wait_recv()

    first_column = me * strip - P_SIZE
    column = lax.broadcasted_iota(jnp.int32, (block_rows, LANES), 1)

    arrived(jnp.int32(0))

    def render(i, carry):
        for more in range(1, GROUP + 1):
            arrived(i * GROUP + more)
        group = jnp.where(rising, i, steps - 1 - i)
        start = pl.multiple_of(group * block_rows, block_rows)
        smooth[...] = jnp.dot(
            row_mats[...], recv[pl.ds(start, window), :], preferred_element_type=F32
        ).astype(BF16)
        total = jnp.zeros(((panels + 1) * block_rows, LANES), F32)
        for k in range(NK):
            own = smooth[k * block_rows : (k + 1) * block_rows, :]
            pieces = [jnp.concatenate([own[:, strip:], own[:, :LANES]], axis=1)]
            pieces += [own[:, (p - 1) * LANES : (p + 1) * LANES] for p in range(1, panels + 1)]
            field = jnp.dot(
                jnp.concatenate(pieces, axis=0), column_mats[k], preferred_element_type=F32
            )
            total = total + weight_ref[k] * field * field
        into = pl.multiple_of(EDGE + start, EDGE)
        for p in range(panels + 1):
            part = total[p * block_rows : (p + 1) * block_rows]
            if p in (0, panels):
                at = column + (first_column + p * LANES)
                part = jnp.where(jnp.logical_and(at >= 0, at < width), part, 0.0)
            intensity[pl.ds(into, block_rows), p * LANES : (p + 1) * LANES] = part.astype(BF16)
        return carry

    lax.fori_loop(0, steps, render, 0)

    fetch.wait()

    def warp(b, carry):
        u = table[pl.ds(phase_ref[0, b, 0], 1), : 2 * IH]
        v = table[pl.ds(phase_ref[1, b, 0], 1), : 2 * IH]
        row_matrix = banded_rows(
            EDGE + 1 - IH + shift_ref[0, b, 0], u, (BLK, BLK + 2 * EDGE)
        ).astype(BF16)
        column_matrix = banded(
            P_SIZE + 1 - IH + shift_ref[1, b, 0], v, (2 * LANES, LANES)
        ).astype(BF16)
        start = pl.multiple_of(b * BLK, BLK)
        partial = jnp.dot(
            row_matrix, intensity[pl.ds(start, BLK + 2 * EDGE), :], preferred_element_type=F32
        ).astype(BF16)
        pieces = [partial[:, p * LANES : (p + 2) * LANES] for p in range(panels)]
        warped = jnp.dot(
            jnp.concatenate(pieces, axis=0), column_matrix, preferred_element_type=F32
        )
        care = care_ref[b, 0].astype(F32)
        for p in range(panels):
            measured = image[pl.ds(start, BLK), p * LANES : (p + 1) * LANES].astype(F32)
            diff[pl.ds(pl.multiple_of(8 + start, 8), BLK), p * LANES : (p + 1) * LANES] = care * (
                measured - warped[p * BLK : (p + 1) * BLK]
            )
        return carry

    lax.fori_loop(0, height // BLK, warp, 0)

    part_rows = 32

    def stencil(i, carry):
        first, second = carry
        start = pl.multiple_of(i * part_rows, part_rows)
        around = diff[pl.ds(start, part_rows + 16), :]
        middle = around[8 : 8 + part_rows]
        value = middle + 0.5 * (around[7 : 7 + part_rows] + around[9 : 9 + part_rows])
        filt[pl.ds(start, part_rows), :] = value
        square = value * value
        for r in range(0, part_rows, 8):
            for p in range(panels):
                first = first + value[r : r + 8, p * LANES : (p + 1) * LANES]
                second = second + square[r : r + 8, p * LANES : (p + 1) * LANES]
        return first, second

    none = jnp.zeros((8, LANES), F32)
    first, second = lax.fori_loop(0, height // part_rows, stencil, (none, none))
    stats_mine[:8, :] = first
    stats_mine[8:, :] = second

    def stat_to(peer):
        return pltpu.make_async_remote_copy(
            src_ref=stats_mine,
            dst_ref=stats_all.at[me],
            send_sem=stat_send.at[peer],
            recv_sem=stat_recv.at[me],
            device_id={"band": peer},
            device_id_type=pl.DeviceIdType.MESH,
        )

    def stat_from(peer):
        return pltpu.make_async_remote_copy(
            src_ref=stats_mine,
            dst_ref=stats_all.at[peer],
            send_sem=stat_send.at[peer],
            recv_sem=stat_recv.at[peer],
            device_id={"band": peer},
            device_id_type=pl.DeviceIdType.MESH,
        )

    def send_stats(i, carry):
        peer = lax.rem(me + n // 2 + i, n)

        @pl.when(peer != me)
        def _():
            stat_to(peer).start()

        return carry

    lax.fori_loop(0, n, send_stats, 0)
    stats_all[me] = stats_mine[...]

    def finish_sends(i, carry):
        peer = lax.rem(me + i, n)
        copy_to(peer).wait_send()
        return carry

    lax.fori_loop(1, n, finish_sends, 0)

    def take_stats(i, carry):
        peer = lax.rem(me + i, n)
        stat_from(peer).wait_recv()
        stat_to(peer).wait_send()
        return carry

    lax.fori_loop(1, n, take_stats, 0)

    sums = lax.fori_loop(
        0, n, lambda i, carry: carry + stats_all[i], jnp.zeros((16, LANES), F32)
    )
    cells = height * width
    mean = jnp.sum(jnp.sum(sums[:8], axis=1, keepdims=True), axis=0, keepdims=True) / cells
    power = jnp.sum(jnp.sum(sums[8:], axis=1, keepdims=True), axis=0, keepdims=True) / cells
    scale = lax.rsqrt(power - mean * mean + epsilon)

    per_block = BLK // part_rows

    def normalize(i, carry):
        start = pl.multiple_of(i * part_rows, part_rows)
        care = care_ref[i // per_block, 0].astype(F32)
        value = filt[pl.ds(start, part_rows), :]
        out_ref[pl.ds(start, part_rows), :] = (care * ((value - mean) * scale)).astype(BF16)
        return carry

    lax.fori_loop(0, height // part_rows, normalize, 0)


def on_device(
    design, row_taps, column_taps, kernel_weight, interp, block_shift, block_phase, care, image
):
    n = lax.axis_size("band")
    rows, width = design.shape
    height, strip = image.shape
    wide = strip + LANES
    block_rows = GROUP * rows
    window = block_rows + 2 * KH
    smem = pl.BlockSpec(memory_space=pltpu.SMEM)
    vmem = pl.BlockSpec(memory_space=pltpu.VMEM)
    return pl.pallas_call(
        functools.partial(kernel, n, height, width),
        out_shape=jax.ShapeDtypeStruct((height, strip), BF16),
        in_specs=[smem] * 4 + [vmem] * 4 + [pl.BlockSpec(memory_space=pl.ANY)],
        out_specs=vmem,
        scratch_shapes=[
            pltpu.VMEM((n, rows, wide), BF16),
            pltpu.VMEM((height + 2 * KH, wide), BF16),
            pltpu.VMEM((height, strip), BF16),
            pltpu.VMEM((NK * block_rows, window), BF16),
            pltpu.VMEM((NK, 2 * LANES, LANES), BF16),
            pltpu.VMEM((2 * NK, LANES), F32),
            pltpu.VMEM((interp.shape[0], LANES), F32),
            pltpu.VMEM((NK * block_rows, wide), BF16),
            pltpu.VMEM((height + 2 * EDGE, wide), BF16),
            pltpu.VMEM((height + 16, strip), F32),
            pltpu.VMEM((height, strip), F32),
            pltpu.VMEM((16, LANES), F32),
            pltpu.VMEM((n, 16, LANES), F32),
            pltpu.SemaphoreType.DMA((n,)),
            pltpu.SemaphoreType.DMA((n,)),
            pltpu.SemaphoreType.DMA((n,)),
            pltpu.SemaphoreType.DMA((n,)),
            pltpu.SemaphoreType.DMA,
        ],
        compiler_params=pltpu.CompilerParams(collective_id=0, has_side_effects=True),
    )(
        kernel_weight, block_shift, block_phase, care,
        design, row_taps, column_taps, interp, image,
    )


def solution(mesh):
    placed = (
        P(("swath", "band"), None),
        P(),
        P(),
        P(),
        P(),
        P(None, "swath", "band"),
        P(None, "swath", "band"),
        P("swath", "band"),
        P("swath", "band"),
    )
    return jax.shard_map(
        on_device, mesh=mesh, in_specs=placed, out_specs=P("swath", "band"), check_vma=False
    )
```

time: 196 us -> 37.8 us (0.19)
  local copies, waits for them, and re-layouts: 73.8 us -> 5.24 us
  matrix products: 34.7 us -> 0 us
  blocking collectives: 32.8 us -> 0 us
  Pallas kernels: 0 us -> 32.3 us
  starting transfers between devices: 19.2 us -> 0 us
  other arithmetic: 18.7 us -> 0 us
  waiting for transfers between devices: 11.7 us -> 0 us
  between operations: 3.08 us -> 0.01 us
    dot_general x21 -> x0, matrix products: 34.7 us -> none  [the longest x8 19.4 us: on_device(): jnp.einsum('rnj,jc->rnc', stacked, column_mats[kernel], preferred_element...]
    psum x1 -> x0, blocking collectives: 32.8 us -> none  [on_device(): lax.psum((jnp.sum(filtered), jnp.sum(filtered * filtered)), 'band')]
    pallas_call x0 -> x1, Pallas kernels: none -> 32.3 us  [on_device(): pl.pallas_call(functools.partial(kernel, n, height, width), out_shape=jax...]
    unnamed x64 -> x11, local copies, waits for them, and re-layouts: 30.6 us -> 5.24 us
    slice x24 -> x0, local copies, waits for them, and re-layouts: 20.8 us -> none  [the longest x8 9.68 us: on_device(): framed[:, :-2, panel - KH:]]
    reshape x16 -> x0, local copies, waits for them, and re-layouts: 18.2 us -> none  [the longest x8 16.2 us: on_device(): field = jnp.einsum('rnj,jc->rnc', stacked, column_mats[kernel], preferred...]
    convert_element_type x3 -> x0, other arithmetic: 14.9 us -> none  [the longest x1 13.3 us: on_device(): intensity = total.astype(jnp.bfloat16)]
    all_to_all x1 -> x0, waiting for transfers between devices: 11.2 us -> none  [on_device(): lax.all_to_all(intensity, 'band', split_axis=1, concat_axis=0, tiled=True)]
  transfers between devices with their start and end apart: 5 -> 0, of which waited for: 2 -> 0; matrix products, arithmetic and copies ran while one was open for 6% -> 0% of each run, Pallas kernels for 0% -> 0%
where the time goes in v1:
time: 37.8 us; the launch traced here: 37.6 us
  Pallas kernels  32.3 us (85%)
  local copies, waits for them, and re-layouts  5.24 us (14%)
    pallas_call x1, Pallas kernels, on_device(): pl.pallas_call(functools.partial(kernel, n, height, width), out_shape=jax...  32.3 us
    unnamed x11, local copies, waits for them, and re-layouts  5.24 us

profile of v1, /device:TPU:0, one launch (start us, length us, event | category | flops | bytes accessed | tf_op | source)
XLA Modules:
  0.0 37.6 jit_solution(193484979915435214)
XLA Ops:
  0.0 0.0 copy-start.1
  0.0 1.3 %copy.12.care_ref = s32[2,1]{1,0:T(2,128)} copy(s32[2,1]{0,1:T(1,128)} %param.16) | data formatting | bytes 16 | tf_op args[7]
  1.3 0.0 copy-done.1
  1.3 0.0 copy-start.2
  1.3 0.7 %copy.10.shift_ref = s32[2,2,1]{2,1,0:T(2,128)} copy(s32[2,2,1]{1,2,0:T(1,128)S(1)} %copy-done.1) | data formatting | bytes 32 | tf_op args[5]
  2.0 0.0 copy-done.2
  2.0 0.0 copy-start
  2.0 0.7 %copy.11.phase_ref = s32[2,2,1]{2,1,0:T(2,128)} copy(s32[2,2,1]{1,2,0:T(1,128)S(1)} %copy-done.2) | data formatting | bytes 32 | tf_op args[6]
  2.7 0.0 copy-done
  2.7 0.7 %copy.13.interp_ref = bf16[32,8]{1,0:T(8,128)(2,1)} copy(bf16[32,8]{0,1:T(8,128)(2,1)S(1)} %copy-done) | data formatting | bytes 1024 | tf_op args[4]
  3.4 32.3 %shard_map.91 = bf16[256,1024]{1,0:T(8,128)(2,1)} custom-call(f32[8]{0:T(128)} %weight_ref.1, s32[2,2,1]{2,1,0:T(2,128)} %copy.10.shift_ref, s32[2,2,1]{2,1,0:T(2,128)} %copy.11.phase_ref, s32[2,1]{1,0:T(2,128)} %copy.12.care_ref, bf16[16,16384]{1,0:T(8,128)(2,1)} %design_ref.1, bf16[8,33]{1,0:T(8,128)(2,1)} %row_ref.1, bf16[8,33]{1,0:T(8,128)(2,1)} %column_ref.1, ...), custom_call_target="tpu_custom_call" | custom-call | tf_op jit(solution)/shard_map/pallas_call | solution.py:317
  35.7 1.9 %copy.15 = bf16[256,1024]{1,0:T(8,128)(2,1)} copy(bf16[256,1024]{1,0:T(8,128)(2,1)} %shard_map.91) | data formatting | bytes 1048576
Async XLA Ops:
  0.0 1.3 %copy-start.1 = (s32[2,2,1]{1,2,0:T(1,128)S(1)}, s32[2,2,1]{1,2,0:T(1,128)}, u32[]{:S(2)}) copy-start(s32[2,2,1]{1,2,0:T(1,128)} %param.14) | copy-start | bytes 52
  1.3 0.7 %copy-start.2 = (s32[2,2,1]{1,2,0:T(1,128)S(1)}, s32[2,2,1]{1,2,0:T(1,128)}, u32[]{:S(2)}) copy-start(s32[2,2,1]{1,2,0:T(1,128)} %param.15) | copy-start | bytes 52
  2.0 0.7 %copy-start = (bf16[32,8]{0,1:T(8,128)(2,1)S(1)}, bf16[32,8]{0,1:T(8,128)(2,1)}, u32[]{:S(2)}) copy-start(bf16[32,8]{0,1:T(8,128)(2,1)} %param.13) | copy-start | bytes 1540

commit v2 on v1

--- a/solution.py
+++ b/solution.py
@@ -14,6 +14,7 @@
 P_SIZE = 28
 LANES = 128
 EDGE = 32
+PART = 32
 GROUP = 4
 REACH = 2 * KH + 1
 
@@ -29,8 +30,8 @@
         - offset
     )
     matrix = jnp.zeros(shape, F32)
-    for tap in range(taps.shape[1]):
-        matrix = jnp.where(place == tap, taps[:, tap : tap + 1], matrix)
+    for tap, value in enumerate(taps):
+        matrix = jnp.where(place == tap, value, matrix)
     return matrix
 
 
@@ -41,19 +42,21 @@
         - offset
     )
     matrix = jnp.zeros(shape, F32)
-    for tap in range(taps.shape[1]):
-        matrix = jnp.where(place == tap, taps[:, tap : tap + 1], matrix)
+    for tap, value in enumerate(taps):
+        matrix = jnp.where(place == tap, value, matrix)
     return matrix
 
 
 def kernel(
     n, height, width,
+    weight_hbm, shift_hbm, phase_hbm, care_hbm,
+    design_hbm, row_hbm, column_hbm, interp_hbm, image_hbm,
+    filt_hbm, mean_ref, scale_ref,
     weight_ref, shift_ref, phase_ref, care_ref,
-    design_ref, row_ref, column_ref, interp_ref, image_hbm,
-    out_ref,
+    design_ref, row_ref, column_ref, interp_ref,
     sendbuf, recv, image, row_mats, column_mats, taps, table, smooth, intensity,
     diff, filt, stats_mine, stats_all,
-    send_sem, recv_sem, stat_send, stat_recv, image_sem,
+    send_sem, recv_sem, stat_send, stat_recv, load_sem, store_sem,
 ):
     me = lax.axis_index("band")
     rows = design_ref.shape[0]
@@ -75,8 +78,25 @@
 
     lax.fori_loop(1, n, greet, 0)
 
-    fetch = pltpu.make_async_copy(image_hbm, image, image_sem)
-    fetch.start()
+    loads = [
+        pltpu.make_async_copy(source, target, load_sem.at[i])
+        for i, (source, target) in enumerate(
+            [
+                (design_hbm, design_ref),
+                (row_hbm, row_ref),
+                (column_hbm, column_ref),
+                (interp_hbm, interp_ref),
+                (weight_hbm, weight_ref),
+                (shift_hbm, shift_ref),
+                (phase_hbm, phase_ref),
+                (care_hbm, care_ref),
+                (image_hbm, image),
+            ]
+        )
+    ]
+    for load in loads:
+        load.start()
+    loads[0].wait()
 
     lane = lax.broadcasted_iota(jnp.int32, (rows, LANES), 1)
     low = lane < LANES // 2
@@ -111,15 +131,17 @@
         )
 
     def send(i, carry):
-        peer = lax.rem(me + n // 2 + i, n)
-
-        @pl.when(peer != me)
+        @pl.when(me + i < n)
         def _():
-            copy_to(peer).start()
-
-        return carry
-
-    lax.fori_loop(0, n, send, 0)
+            copy_to(me + i).start()
+
+        @pl.when(me - i >= 0)
+        def _():
+            copy_to(me - i).start()
+
+        return carry
+
+    lax.fori_loop(1, n, send, 0)
 
     recv[pl.ds(pl.multiple_of(KH + me * rows, rows), rows), :] = sendbuf[me]
     recv[:KH, :] = jnp.zeros((KH, wide), BF16)
@@ -129,16 +151,23 @@
     diff[:8, :] = jnp.zeros((8, strip), F32)
     diff[8 + height :, :] = jnp.zeros((8, strip), F32)
 
+    for load in loads[1:-1]:
+        load.wait()
     taps[:NK, :REACH] = row_ref[...].astype(F32)
     taps[NK:, :REACH] = column_ref[...].astype(F32)
-    table[:, : 2 * IH] = interp_ref[...].astype(F32)
+    table[...] = interp_ref[...].astype(F32)
+    phases = lax.broadcasted_iota(jnp.int32, table.shape, 1)
+
+    def chosen(phase):
+        row = jnp.sum(jnp.where(phases == phase, table[...], 0.0), axis=1, keepdims=True)
+        return [row[t : t + 1] for t in range(2 * IH)]
 
     def build(k, carry):
-        row_taps = taps[pl.ds(k, 1), :REACH]
+        row_taps = [taps[pl.ds(k, 1), t : t + 1] for t in range(REACH)]
         row_mats[pl.ds(pl.multiple_of(k * block_rows, block_rows), block_rows), :] = banded_rows(
             0, row_taps, (block_rows, window)
         ).astype(BF16)
-        column_taps = taps[pl.ds(NK + k, 1), :REACH]
+        column_taps = [taps[pl.ds(NK + k, 1), t : t + 1] for t in range(REACH)]
         column_mats[k] = banded(LANES - P_SIZE - KH, column_taps, (2 * LANES, LANES)).astype(BF16)
         return carry
 
@@ -156,7 +185,10 @@
     first_column = me * strip - P_SIZE
     column = lax.broadcasted_iota(jnp.int32, (block_rows, LANES), 1)
 
-    arrived(jnp.int32(0))
+    per_block = BLK // block_rows
+    count = height // BLK
+    part_rows = PART
+    parts = BLK // part_rows
 
     def render(i, carry):
         for more in range(1, GROUP + 1):
@@ -182,20 +214,22 @@
                 at = column + (first_column + p * LANES)
                 part = jnp.where(jnp.logical_and(at >= 0, at < width), part, 0.0)
             intensity[pl.ds(into, block_rows), p * LANES : (p + 1) * LANES] = part.astype(BF16)
-        return carry
-
-    lax.fori_loop(0, steps, render, 0)
-
-    fetch.wait()
-
-    def warp(b, carry):
-        u = table[pl.ds(phase_ref[0, b, 0], 1), : 2 * IH]
-        v = table[pl.ds(phase_ref[1, b, 0], 1), : 2 * IH]
+
+        @pl.when(jnp.logical_and(i >= per_block, lax.rem(i, per_block) == 0))
+        def _():
+            warp(i // per_block - 1)
+
+        return carry
+
+    def warp(place):
+        b = jnp.where(rising, place, count - 1 - place)
+        u = chosen(phase_ref[0, 0, b])
+        v = chosen(phase_ref[1, 0, b])
         row_matrix = banded_rows(
-            EDGE + 1 - IH + shift_ref[0, b, 0], u, (BLK, BLK + 2 * EDGE)
+            EDGE + 1 - IH + shift_ref[0, 0, b], u, (BLK, BLK + 2 * EDGE)
         ).astype(BF16)
         column_matrix = banded(
-            P_SIZE + 1 - IH + shift_ref[1, b, 0], v, (2 * LANES, LANES)
+            P_SIZE + 1 - IH + shift_ref[1, 0, b], v, (2 * LANES, LANES)
         ).astype(BF16)
         start = pl.multiple_of(b * BLK, BLK)
         partial = jnp.dot(
@@ -205,36 +239,45 @@
         warped = jnp.dot(
             jnp.concatenate(pieces, axis=0), column_matrix, preferred_element_type=F32
         )
-        care = care_ref[b, 0].astype(F32)
+        care = care_ref[0, b].astype(F32)
         for p in range(panels):
             measured = image[pl.ds(start, BLK), p * LANES : (p + 1) * LANES].astype(F32)
             diff[pl.ds(pl.multiple_of(8 + start, 8), BLK), p * LANES : (p + 1) * LANES] = care * (
                 measured - warped[p * BLK : (p + 1) * BLK]
             )
-        return carry
-
-    lax.fori_loop(0, height // BLK, warp, 0)
-
-    part_rows = 32
-
-    def stencil(i, carry):
-        first, second = carry
-        start = pl.multiple_of(i * part_rows, part_rows)
+
+        first_part = place * parts - jnp.where(place > 0, 1, 0)
+        last_part = (place + 1) * parts - jnp.where(place < count - 1, 1, 0)
+        lax.fori_loop(first_part, last_part, stencil, 0)
+
+    def store(part):
+        where = pl.ds(pl.multiple_of(part * part_rows, part_rows), part_rows)
+        return pltpu.make_async_copy(filt.at[where], filt_hbm.at[where], store_sem.at[part])
+
+    def stencil(place, carry):
+        part = jnp.where(rising, place, count * parts - 1 - place)
+        start = pl.multiple_of(part * part_rows, part_rows)
         around = diff[pl.ds(start, part_rows + 16), :]
         middle = around[8 : 8 + part_rows]
         value = middle + 0.5 * (around[7 : 7 + part_rows] + around[9 : 9 + part_rows])
         filt[pl.ds(start, part_rows), :] = value
+        store(part).start()
         square = value * value
+        first = stats_mine[:8, :]
+        second = stats_mine[8:, :]
         for r in range(0, part_rows, 8):
             for p in range(panels):
                 first = first + value[r : r + 8, p * LANES : (p + 1) * LANES]
                 second = second + square[r : r + 8, p * LANES : (p + 1) * LANES]
-        return first, second
-
-    none = jnp.zeros((8, LANES), F32)
-    first, second = lax.fori_loop(0, height // part_rows, stencil, (none, none))
-    stats_mine[:8, :] = first
-    stats_mine[8:, :] = second
+        stats_mine[:8, :] = first
+        stats_mine[8:, :] = second
+        return carry
+
+    loads[-1].wait()
+    stats_mine[...] = jnp.zeros((16, LANES), F32)
+    arrived(jnp.int32(0))
+    lax.fori_loop(0, steps, render, 0)
+    warp(jnp.int32(count - 1))
 
     def stat_to(peer):
         return pltpu.make_async_remote_copy(
@@ -290,17 +333,15 @@
     mean = jnp.sum(jnp.sum(sums[:8], axis=1, keepdims=True), axis=0, keepdims=True) / cells
     power = jnp.sum(jnp.sum(sums[8:], axis=1, keepdims=True), axis=0, keepdims=True) / cells
     scale = lax.rsqrt(power - mean * mean + epsilon)
-
-    per_block = BLK // part_rows
-
-    def normalize(i, carry):
-        start = pl.multiple_of(i * part_rows, part_rows)
-        care = care_ref[i // per_block, 0].astype(F32)
-        value = filt[pl.ds(start, part_rows), :]
-        out_ref[pl.ds(start, part_rows), :] = (care * ((value - mean) * scale)).astype(BF16)
-        return carry
-
-    lax.fori_loop(0, height // part_rows, normalize, 0)
+    mean_ref[...] = jnp.broadcast_to(mean, (1, strip))
+    for b in range(count):
+        scale_ref[b : b + 1, :] = jnp.broadcast_to(care_ref[0, b].astype(F32) * scale, (1, strip))
+
+    def finish_store(part, carry):
+        store(part).wait()
+        return carry
+
+    lax.fori_loop(0, count * parts, finish_store, 0)
 
 
 def on_device(
@@ -312,21 +353,34 @@
     wide = strip + LANES
     block_rows = GROUP * rows
     window = block_rows + 2 * KH
-    smem = pl.BlockSpec(memory_space=pltpu.SMEM)
+    count = height // BLK
+    hbm = pl.BlockSpec(memory_space=pltpu.HBM)
     vmem = pl.BlockSpec(memory_space=pltpu.VMEM)
-    return pl.pallas_call(
+    filtered, mean, scale = pl.pallas_call(
         functools.partial(kernel, n, height, width),
-        out_shape=jax.ShapeDtypeStruct((height, strip), BF16),
-        in_specs=[smem] * 4 + [vmem] * 4 + [pl.BlockSpec(memory_space=pl.ANY)],
-        out_specs=vmem,
+        out_shape=(
+            jax.ShapeDtypeStruct((height, strip), F32),
+            jax.ShapeDtypeStruct((1, strip), F32),
+            jax.ShapeDtypeStruct((count, strip), F32),
+        ),
+        in_specs=[hbm] * 9,
+        out_specs=(hbm, vmem, vmem),
         scratch_shapes=[
+            pltpu.SMEM((NK,), F32),
+            pltpu.SMEM((2, 1, count), jnp.int32),
+            pltpu.SMEM((2, 1, count), jnp.int32),
+            pltpu.SMEM((1, count), jnp.int32),
+            pltpu.VMEM((rows, width), BF16),
+            pltpu.VMEM(row_taps.shape, BF16),
+            pltpu.VMEM(column_taps.shape, BF16),
+            pltpu.VMEM(interp.shape[::-1], BF16),
             pltpu.VMEM((n, rows, wide), BF16),
             pltpu.VMEM((height + 2 * KH, wide), BF16),
             pltpu.VMEM((height, strip), BF16),
             pltpu.VMEM((NK * block_rows, window), BF16),
             pltpu.VMEM((NK, 2 * LANES, LANES), BF16),
             pltpu.VMEM((2 * NK, LANES), F32),
-            pltpu.VMEM((interp.shape[0], LANES), F32),
+            pltpu.VMEM(interp.shape[::-1], F32),
             pltpu.VMEM((NK * block_rows, wide), BF16),
             pltpu.VMEM((height + 2 * EDGE, wide), BF16),
             pltpu.VMEM((height + 16, strip), F32),
@@ -337,13 +391,24 @@
             pltpu.SemaphoreType.DMA((n,)),
             pltpu.SemaphoreType.DMA((n,)),
             pltpu.SemaphoreType.DMA((n,)),
-            pltpu.SemaphoreType.DMA,
+            pltpu.SemaphoreType.DMA((9,)),
+            pltpu.SemaphoreType.DMA((height // PART,)),
         ],
         compiler_params=pltpu.CompilerParams(collective_id=0, has_side_effects=True),
     )(
-        kernel_weight, block_shift, block_phase, care,
-        design, row_taps, column_taps, interp, image,
-    )
+        kernel_weight,
+        jnp.transpose(block_shift, (0, 2, 1)),
+        jnp.transpose(block_phase, (0, 2, 1)),
+        care.T,
+        design,
+        row_taps,
+        column_taps,
+        interp.T,
+        image,
+    )
+    blocks = filtered.reshape(count, BLK, strip)
+    out = (blocks - mean[:, None]) * scale[:, None]
+    return out.reshape(height, strip).astype(BF16)
 
 
 def solution(mesh):

time: 37.8 us -> 34.7 us (0.918)
  local copies, waits for them, and re-layouts: 5.24 us -> 0.67 us
  other arithmetic: 0 us -> 2.15 us
  Pallas kernels: 32.3 us -> 31.7 us
    unnamed x11 -> x2, local copies, waits for them, and re-layouts: 5.24 us -> 0.67 us
    convert_element_type x0 -> x1, other arithmetic: none -> 2.15 us  [on_device(): return out.reshape(height, strip).astype(BF16)]
    pallas_call x1, Pallas kernels: 32.3 us -> 31.7 us  [on_device(): pl.pallas_call(functools.partial(kernel, n, height, width), out_shape=(ja...]
where the time goes in v2:
time: 34.7 us; the launch traced here: 34.5 us
  Pallas kernels  31.7 us (91%)
  other arithmetic  2.15 us (6%)
  local copies, waits for them, and re-layouts  0.67 us (2%)
    pallas_call x1, Pallas kernels, on_device(): pl.pallas_call(functools.partial(kernel, n, height, width), out_shape=(ja...  31.7 us
    convert_element_type x1, other arithmetic, on_device(): return out.reshape(height, strip).astype(BF16)  2.15 us

profile of v2, /device:TPU:0, one launch (start us, length us, event | category | flops | bytes accessed | tf_op | source)
XLA Modules:
  0.0 34.5 jit_solution(7550640800224254777)
XLA Ops:
  0.0 31.7 %shard_map.91 = (f32[256,1024]{1,0:T(8,128)}, f32[1,1024]{1,0:T(1,128)}, f32[2,1024]{1,0:T(2,128)}) custom-call(f32[8]{0:T(128)} %weight_hbm.1, s32[2,1,2]{2,1,0:T(1,128)} %bitcast.15, s32[2,1,2]{2,1,0:T(1,128)} %bitcast.16, s32[1,2]{1,0:T(1,128)} %bitcast.17, bf16[16,16384]{1,0:T(8,128)(2,1)} %design_hbm.1, bf16[8,33]{1,0:T(8,128)(2,1)} %row_hbm.1, ...), custom_call_target="tpu_custom_call" | custom-call | tf_op jit(solution)/shard_map/pallas_call | solution.py:359
  31.7 0.0 copy-start
  31.7 0.7 %copy-done = f32[1,1024]{1,0:T(1,128)S(1)} copy-done((f32[1,1024]{1,0:T(1,128)S(1)}, f32[1,1024]{1,0:T(1,128)}, u32[]{:S(2)}) %copy-start) | copy-done | bytes 4120
  32.4 2.1 %fusion = bf16[256,1024]{1,0:T(8,128)(2,1)} fusion(f32[256,1024]{1,0:T(8,128)} %get-tuple-element.8, f32[2,1024]{1,0:T(2,128)} %get-tuple-element.10, f32[1024]{0:T(1024)S(1)} %bitcast.13), kind=kLoop, calls=%fused_computation.1 | loop fusion | flops 786432 | bytes 1585152 | tf_op jit(solution)/shard_map/convert_element_type | solution.py:411
Async XLA Ops:
  31.7 0.7 %copy-start = (f32[1,1024]{1,0:T(1,128)S(1)}, f32[1,1024]{1,0:T(1,128)}, u32[]{:S(2)}) copy-start(f32[1,1024]{1,0:T(1,128)} %get-tuple-element.9) | copy-start | bytes 12292

commit v3 on v2

--- a/solution.py
+++ b/solution.py
@@ -19,6 +19,9 @@
 REACH = 2 * KH + 1
 
 epsilon = 1e-05
+def pin(x):
+    return pltpu.with_memory_space_constraint(x, pltpu.HBM)
+
 F32 = jnp.float32
 BF16 = jnp.bfloat16
 
@@ -51,12 +54,12 @@
     n, height, width,
     weight_hbm, shift_hbm, phase_hbm, care_hbm,
     design_hbm, row_hbm, column_hbm, interp_hbm, image_hbm,
-    filt_hbm, mean_ref, scale_ref,
+    filt, mean_ref, scale_ref,
     weight_ref, shift_ref, phase_ref, care_ref,
     design_ref, row_ref, column_ref, interp_ref,
     sendbuf, recv, image, row_mats, column_mats, taps, table, smooth, intensity,
-    diff, filt, stats_mine, stats_all,
-    send_sem, recv_sem, stat_send, stat_recv, load_sem, store_sem,
+    diff, stats_mine, stats_all,
+    send_sem, recv_sem, stat_send, stat_recv, load_sem,
 ):
     me = lax.axis_index("band")
     rows = design_ref.shape[0]
@@ -250,10 +253,6 @@
         last_part = (place + 1) * parts - jnp.where(place < count - 1, 1, 0)
         lax.fori_loop(first_part, last_part, stencil, 0)
 
-    def store(part):
-        where = pl.ds(pl.multiple_of(part * part_rows, part_rows), part_rows)
-        return pltpu.make_async_copy(filt.at[where], filt_hbm.at[where], store_sem.at[part])
-
     def stencil(place, carry):
         part = jnp.where(rising, place, count * parts - 1 - place)
         start = pl.multiple_of(part * part_rows, part_rows)
@@ -261,7 +260,6 @@
         middle = around[8 : 8 + part_rows]
         value = middle + 0.5 * (around[7 : 7 + part_rows] + around[9 : 9 + part_rows])
         filt[pl.ds(start, part_rows), :] = value
-        store(part).start()
         square = value * value
         first = stats_mine[:8, :]
         second = stats_mine[8:, :]
@@ -336,12 +334,6 @@
     mean_ref[...] = jnp.broadcast_to(mean, (1, strip))
     for b in range(count):
         scale_ref[b : b + 1, :] = jnp.broadcast_to(care_ref[0, b].astype(F32) * scale, (1, strip))
-
-    def finish_store(part, carry):
-        store(part).wait()
-        return carry
-
-    lax.fori_loop(0, count * parts, finish_store, 0)
 
 
 def on_device(
@@ -364,7 +356,7 @@
             jax.ShapeDtypeStruct((count, strip), F32),
         ),
         in_specs=[hbm] * 9,
-        out_specs=(hbm, vmem, vmem),
+        out_specs=(vmem, vmem, vmem),
         scratch_shapes=[
             pltpu.SMEM((NK,), F32),
             pltpu.SMEM((2, 1, count), jnp.int32),
@@ -384,7 +376,6 @@
             pltpu.VMEM((NK * block_rows, wide), BF16),
             pltpu.VMEM((height + 2 * EDGE, wide), BF16),
             pltpu.VMEM((height + 16, strip), F32),
-            pltpu.VMEM((height, strip), F32),
             pltpu.VMEM((16, LANES), F32),
             pltpu.VMEM((n, 16, LANES), F32),
             pltpu.SemaphoreType.DMA((n,)),
@@ -392,19 +383,20 @@
             pltpu.SemaphoreType.DMA((n,)),
             pltpu.SemaphoreType.DMA((n,)),
             pltpu.SemaphoreType.DMA((9,)),
-            pltpu.SemaphoreType.DMA((height // PART,)),
         ],
-        compiler_params=pltpu.CompilerParams(collective_id=0, has_side_effects=True),
+        compiler_params=pltpu.CompilerParams(
+            collective_id=0, has_side_effects=True, vmem_limit_bytes=32 * 1024 * 1024
+        ),
     )(
-        kernel_weight,
-        jnp.transpose(block_shift, (0, 2, 1)),
-        jnp.transpose(block_phase, (0, 2, 1)),
-        care.T,
-        design,
-        row_taps,
-        column_taps,
-        interp.T,
-        image,
+        pin(kernel_weight),
+        pin(jnp.transpose(block_shift, (0, 2, 1))),
+        pin(jnp.transpose(block_phase, (0, 2, 1))),
+        pin(care.T),
+        pin(design),
+        pin(row_taps),
+        pin(column_taps),
+        pin(interp.T),
+        pin(image),
     )
     blocks = filtered.reshape(count, BLK, strip)
     out = (blocks - mean[:, None]) * scale[:, None]

time: 34.7 us -> 32.1 us (0.925)
  other arithmetic: 2.15 us -> 0.92 us
  Pallas kernels: 31.7 us -> 31 us
  local copies, waits for them, and re-layouts: 0.67 us -> 0 us
    convert_element_type x1, other arithmetic: 2.15 us -> 0.92 us  [on_device(): return out.reshape(height, strip).astype(BF16)]
    pallas_call x1, Pallas kernels: 31.7 us -> 31 us  [on_device(): pl.pallas_call(functools.partial(kernel, n, height, width), out_shape=(ja...]
    unnamed x2 -> x0, local copies, waits for them, and re-layouts: 0.67 us -> none
where the time goes in v3:
time: 32.1 us; the launch traced here: 31.9 us
  Pallas kernels  31 us (97%)
  other arithmetic  0.92 us (3%)
    pallas_call x1, Pallas kernels, on_device(): pl.pallas_call(functools.partial(kernel, n, height, width), out_shape=(ja...  31 us
    convert_element_type x1, other arithmetic, on_device(): return out.reshape(height, strip).astype(BF16)  0.92 us

profile of v3, /device:TPU:0, one launch (start us, length us, event | category | flops | bytes accessed | tf_op | source)
XLA Modules:
  0.0 31.9 jit_solution(17910900492070181440)
XLA Ops:
  0.0 31.0 %shard_map.91 = (f32[256,1024]{1,0:T(8,128)S(1)}, f32[1,1024]{1,0:T(1,128)S(1)}, f32[2,1024]{1,0:T(2,128)S(1)}) custom-call(f32[8]{0:T(128)} %weight_hbm.1, s32[2,1,2]{2,1,0:T(1,128)} %bitcast.15, s32[2,1,2]{2,1,0:T(1,128)} %bitcast.16, s32[1,2]{1,0:T(1,128)} %bitcast.17, bf16[16,16384]{1,0:T(8,128)(2,1)} %design_hbm.1, bf16[8,33]{1,0:T(8,128)(2,1)} %row_hbm.1, ...), custom_call_target="tpu_custom_call" | custom-call | tf_op jit(solution)/shard_map/pallas_call | solution.py:351
  31.0 0.9 %fusion = bf16[256,1024]{1,0:T(8,128)(2,1)} fusion(f32[256,1024]{1,0:T(8,128)S(1)} %get-tuple-element.8, f32[2,1024]{1,0:T(2,128)S(1)} %get-tuple-element.10, f32[1024]{0:T(1024)S(1)} %bitcast.13), kind=kLoop, calls=%fused_computation.1 | loop fusion | flops 786432 | bytes 1585152 | tf_op jit(solution)/shard_map/convert_element_type | solution.py:403

commit v4 on v3

--- a/solution.py
+++ b/solution.py
@@ -58,7 +58,7 @@
     weight_ref, shift_ref, phase_ref, care_ref,
     design_ref, row_ref, column_ref, interp_ref,
     sendbuf, recv, image, row_mats, column_mats, taps, table, smooth, intensity,
-    diff, stats_mine, stats_all,
+    diff, partial_sums, stats_mine, stats_all,
     send_sem, recv_sem, stat_send, stat_recv, load_sem,
 ):
     me = lax.axis_index("band")
@@ -261,21 +261,23 @@
         value = middle + 0.5 * (around[7 : 7 + part_rows] + around[9 : 9 + part_rows])
         filt[pl.ds(start, part_rows), :] = value
         square = value * value
-        first = stats_mine[:8, :]
-        second = stats_mine[8:, :]
+        first = partial_sums[:8, :]
+        second = partial_sums[8:, :]
         for r in range(0, part_rows, 8):
             for p in range(panels):
                 first = first + value[r : r + 8, p * LANES : (p + 1) * LANES]
                 second = second + square[r : r + 8, p * LANES : (p + 1) * LANES]
-        stats_mine[:8, :] = first
-        stats_mine[8:, :] = second
+        partial_sums[:8, :] = first
+        partial_sums[8:, :] = second
         return carry
 
     loads[-1].wait()
-    stats_mine[...] = jnp.zeros((16, LANES), F32)
+    partial_sums[...] = jnp.zeros((16, LANES), F32)
     arrived(jnp.int32(0))
     lax.fori_loop(0, steps, render, 0)
     warp(jnp.int32(count - 1))
+    stats_mine[0:1, :] = jnp.sum(partial_sums[:8, :], axis=0, keepdims=True)
+    stats_mine[1:2, :] = jnp.sum(partial_sums[8:, :], axis=0, keepdims=True)
 
     def stat_to(peer):
         return pltpu.make_async_remote_copy(
@@ -325,11 +327,11 @@
     lax.fori_loop(1, n, take_stats, 0)
 
     sums = lax.fori_loop(
-        0, n, lambda i, carry: carry + stats_all[i], jnp.zeros((16, LANES), F32)
+        0, n, lambda i, carry: carry + stats_all[i], jnp.zeros((2, LANES), F32)
     )
     cells = height * width
-    mean = jnp.sum(jnp.sum(sums[:8], axis=1, keepdims=True), axis=0, keepdims=True) / cells
-    power = jnp.sum(jnp.sum(sums[8:], axis=1, keepdims=True), axis=0, keepdims=True) / cells
+    mean = jnp.sum(sums[0:1], axis=1, keepdims=True) / cells
+    power = jnp.sum(sums[1:2], axis=1, keepdims=True) / cells
     scale = lax.rsqrt(power - mean * mean + epsilon)
     mean_ref[...] = jnp.broadcast_to(mean, (1, strip))
     for b in range(count):
@@ -377,7 +379,8 @@
             pltpu.VMEM((height + 2 * EDGE, wide), BF16),
             pltpu.VMEM((height + 16, strip), F32),
             pltpu.VMEM((16, LANES), F32),
-            pltpu.VMEM((n, 16, LANES), F32),
+            pltpu.VMEM((2, LANES), F32),
+            pltpu.VMEM((n, 2, LANES), F32),
             pltpu.SemaphoreType.DMA((n,)),
             pltpu.SemaphoreType.DMA((n,)),
             pltpu.SemaphoreType.DMA((n,)),

time: 32.1 us -> 30.9 us (0.963)
  Pallas kernels: 31 us -> 29.8 us
    pallas_call x1, Pallas kernels: 31 us -> 29.8 us  [on_device(): pl.pallas_call(functools.partial(kernel, n, height, width), out_shape=(ja...]
where the time goes in v4:
time: 30.9 us; the launch traced here: 30.8 us
  Pallas kernels  29.8 us (96%)
  other arithmetic  0.92 us (3%)
    pallas_call x1, Pallas kernels, on_device(): pl.pallas_call(functools.partial(kernel, n, height, width), out_shape=(ja...  29.8 us
    convert_element_type x1, other arithmetic, on_device(): return out.reshape(height, strip).astype(BF16)  0.92 us

profile of v4, /device:TPU:0, one launch (start us, length us, event | category | flops | bytes accessed | tf_op | source)
XLA Modules:
  0.0 30.8 jit_solution(14589962721495561539)
XLA Ops:
  0.0 29.8 %shard_map.91 = (f32[256,1024]{1,0:T(8,128)S(1)}, f32[1,1024]{1,0:T(1,128)S(1)}, f32[2,1024]{1,0:T(2,128)S(1)}) custom-call(f32[8]{0:T(128)} %weight_hbm.1, s32[2,1,2]{2,1,0:T(1,128)} %bitcast.15, s32[2,1,2]{2,1,0:T(1,128)} %bitcast.16, s32[1,2]{1,0:T(1,128)} %bitcast.17, bf16[16,16384]{1,0:T(8,128)(2,1)} %design_hbm.1, bf16[8,33]{1,0:T(8,128)(2,1)} %row_hbm.1, ...), custom_call_target="tpu_custom_call" | custom-call | tf_op jit(solution)/shard_map/pallas_call | solution.py:353
  29.8 0.9 %fusion = bf16[256,1024]{1,0:T(8,128)(2,1)} fusion(f32[256,1024]{1,0:T(8,128)S(1)} %get-tuple-element.8, f32[2,1024]{1,0:T(2,128)S(1)} %get-tuple-element.10, f32[1024]{0:T(1024)S(1)} %bitcast.13), kind=kLoop, calls=%fused_computation.1 | loop fusion | flops 786432 | bytes 1585152 | tf_op jit(solution)/shard_map/convert_element_type | solution.py:406
